TPU v7x, 32 devices: a whole 2x2x4 slice. The times are simulated.
32 devices in a mesh: facet: 8 (over z, core), slab: 4 (over y, x).
Axes of the slice: x: 2, y: 2, z: 4, core: 2. Of those that a mesh axis runs over, the one named last changes fastest.
Arguments:
- facets: float32 [8, 256, 4096], P('facet', 'slab'), may hold values from -20 to 20
- row_taper: float32 [256], P('slab'), may hold values from 0.5 to 2
- col_taper: float32 [4096], replicated, may hold values from 0.5 to 2
- facet_offsets: int32 [8, 2], P('facet'), may hold values from 0 to 32767
- col_offsets: int32 [8], replicated, may hold values from 0 to 32767
- row_offsets: int32 [8, 2], replicated, may hold values from 0 to 32767
Outputs:
- subgrids: float32 [2, 8, 2, 128, 128], P(None, 'facet', None, 'slab')
All inputs are finite; a program needn't handle non-finite values.
Results may differ from a plain program's by a relative error of at most 0.0003.
Values sent between devices are 32-bit elements; how exact they have to be, the bound alone decides.
A program may use at most 64 MiB of HBM per device.

v0:
```python
import math

import jax
import jax.numpy as jnp
from jax import lax
from jax.sharding import PartitionSpec as P

GRID = 32768
CONTRIB = 128


def phase_pair(positions, frequency):
    product = positions[:, None] % GRID * (frequency[..., None, :] % GRID) % GRID
    angles = product.astype(jnp.float32) * (2.0 * math.pi / GRID)
    return (jnp.cos(angles), jnp.sin(angles))


def facet_terms(weighted, row_pos, col_pos, col_offsets, row_offsets):
    highest = lax.Precision.HIGHEST
    frequency = jnp.arange(CONTRIB, dtype=jnp.int32)

    def one_column(column):
        col_cos, col_sin = phase_pair(col_pos, frequency + col_offsets[column])
        tables = jnp.concatenate([col_cos, col_sin], axis=1)
        projected = jnp.dot(weighted, tables, precision=highest, preferred_element_type=jnp.float32)
        real_part = projected[:, :CONTRIB]
        imag_part = -projected[:, CONTRIB:]
        row_cos, row_sin = phase_pair(row_pos, frequency[None, :] + row_offsets[column][:, None])
        sub_real = jnp.einsum("qai,aj->qij", row_cos, real_part, precision=highest) + jnp.einsum(
            "qai,aj->qij", row_sin, imag_part, precision=highest
        )
        sub_imag = jnp.einsum("qai,aj->qij", row_cos, imag_part, precision=highest) - jnp.einsum(
            "qai,aj->qij", row_sin, real_part, precision=highest
        )
        return jnp.stack([sub_real, sub_imag])

    stacked = lax.map(one_column, jnp.arange(col_offsets.shape[0], dtype=jnp.int32))
    return jnp.moveaxis(stacked, 0, 1)


def local(facets, row_taper, col_taper, facet_offsets, col_offsets, row_offsets):
    row_count = facets.shape[1]
    width = facets.shape[2]
    groups = lax.axis_size("facet")
    slabs = lax.axis_size("slab")
    columns = col_offsets.shape[0]
    first_row = lax.axis_index("slab") * row_count
    weighted = facets[0] * row_taper[:, None] * col_taper[None, :]
    row_pos = jnp.arange(row_count, dtype=jnp.int32) + first_row + facet_offsets[0, 0]
    col_pos = jnp.arange(width, dtype=jnp.int32) + facet_offsets[0, 1]
    summed = facet_terms(weighted, row_pos, col_pos, col_offsets, row_offsets)
    reduced = lax.psum_scatter(summed, "slab", scatter_dimension=3, tiled=True)
    regrouped = lax.all_to_all(reduced, "facet", split_axis=1, concat_axis=1, tiled=True)
    shape = regrouped.shape
    result = regrouped.reshape((2, groups, columns // groups) + shape[2:]).sum(axis=1)
    scale = 1.0 / math.sqrt(facets.shape[0] * groups * row_count * slabs * width)
    return result * scale


def solution(mesh):
    placed = (P("facet", "slab", None), P("slab"), P(), P("facet", None), P(), P())
    return jax.shard_map(
        local,
        mesh=mesh,
        in_specs=placed,
        out_specs=P(None, "facet", None, "slab", None),
        check_vma=False,
    )
```

profile of v0, /device:TPU:0, one launch (start us, length us, event | category | flops | bytes accessed | tf_op | source)
XLA Modules:
  0.0 223.4 jit_solution(16022564907464864516)
XLA Ops:
  6.5 1.3 fusion.64
  7.9 0.8 copy.7
  8.6 1.4 fusion.63
  10.1 146.4 %while.16 = (s32[]{:T(128)}, f32[8,2,2,128,128]{4,3,2,1,0:T(8,128)S(1)}, s32[8]{0:T(128)S(1)}, s32[8,2]{1,0:T(8,128)S(1)}, s32[8]{0:T(128)S(1)}, /*index=5*/f32[...) while((s32[]{:T(128)}, ...), condition=%wide.region_1.2_spmd.clone.clone.clone, body=%wide.region_0.1_spmd.clone.clone.clone.sunk | while | flops 915477824 | bytes 10985951 | solution.py:37
  14.1 8.2 %fusion.89 = (f32[4096,128]{1,0:T(8,128)S(1)}, f32[4096,128]{1,0:T(8,128)S(1)}) fusion(s32[128]{0:T(128)S(1)} %and_select_fusion.8, s32[4096]{0:T(1024)S(1)} %add_select_fusion.4), kind=kLoop, calls=%fused_computation.23.clone.1 | loop fusion | flops 7340032 | bytes 4211200 | tf_op jit(solution)/shard_map/while/body/eval_jaxpr/cos | solution.py:15
  22.3 2.6 %fusion.90 = f32[64,256]{1,0:T(8,128)S(1)} fusion(f32[64,4096]{1,0:T(8,128)S(1)} %get-tuple-element.379, f32[4096,128]{1,0:T(8,128)S(1)} %get-tuple-element.348, f32[4096,128]{1,0:T(8,128)S(1)} %get-tuple-element.349), kind=kOutput, calls=%fused_computation.21.clone.1 | convolution fusion | flops 806354944 | bytes 5308416 | tf_op jit(solution)/shard_map/while/body/eval_jaxpr/dot_general | solution.py:25
  32.4 8.2 %fusion.89 = (f32[4096,128]{1,0:T(8,128)S(1)}, f32[4096,128]{1,0:T(8,128)S(1)}) fusion(s32[128]{0:T(128)S(1)} %and_select_fusion.8, s32[4096]{0:T(1024)S(1)} %add_select_fusion.4), kind=kLoop, calls=%fused_computation.23.clone.1 | loop fusion | flops 7340032 | bytes 4211200 | tf_op jit(solution)/shard_map/while/body/eval_jaxpr/cos | solution.py:15
  40.6 2.6 %fusion.90 = f32[64,256]{1,0:T(8,128)S(1)} fusion(f32[64,4096]{1,0:T(8,128)S(1)} %get-tuple-element.379, f32[4096,128]{1,0:T(8,128)S(1)} %get-tuple-element.348, f32[4096,128]{1,0:T(8,128)S(1)} %get-tuple-element.349), kind=kOutput, calls=%fused_computation.21.clone.1 | convolution fusion | flops 806354944 | bytes 5308416 | tf_op jit(solution)/shard_map/while/body/eval_jaxpr/dot_general | solution.py:25
  44.6 0.7 fusion.94
  50.7 8.2 %fusion.89 = (f32[4096,128]{1,0:T(8,128)S(1)}, f32[4096,128]{1,0:T(8,128)S(1)}) fusion(s32[128]{0:T(128)S(1)} %and_select_fusion.8, s32[4096]{0:T(1024)S(1)} %add_select_fusion.4), kind=kLoop, calls=%fused_computation.23.clone.1 | loop fusion | flops 7340032 | bytes 4211200 | tf_op jit(solution)/shard_map/while/body/eval_jaxpr/cos | solution.py:15
  58.9 2.6 %fusion.90 = f32[64,256]{1,0:T(8,128)S(1)} fusion(f32[64,4096]{1,0:T(8,128)S(1)} %get-tuple-element.379, f32[4096,128]{1,0:T(8,128)S(1)} %get-tuple-element.348, f32[4096,128]{1,0:T(8,128)S(1)} %get-tuple-element.349), kind=kOutput, calls=%fused_computation.21.clone.1 | convolution fusion | flops 806354944 | bytes 5308416 | tf_op jit(solution)/shard_map/while/body/eval_jaxpr/dot_general | solution.py:25
  62.9 0.7 fusion.94
  69.0 8.2 %fusion.89 = (f32[4096,128]{1,0:T(8,128)S(1)}, f32[4096,128]{1,0:T(8,128)S(1)}) fusion(s32[128]{0:T(128)S(1)} %and_select_fusion.8, s32[4096]{0:T(1024)S(1)} %add_select_fusion.4), kind=kLoop, calls=%fused_computation.23.clone.1 | loop fusion | flops 7340032 | bytes 4211200 | tf_op jit(solution)/shard_map/while/body/eval_jaxpr/cos | solution.py:15
  77.2 2.6 %fusion.90 = f32[64,256]{1,0:T(8,128)S(1)} fusion(f32[64,4096]{1,0:T(8,128)S(1)} %get-tuple-element.379, f32[4096,128]{1,0:T(8,128)S(1)} %get-tuple-element.348, f32[4096,128]{1,0:T(8,128)S(1)} %get-tuple-element.349), kind=kOutput, calls=%fused_computation.21.clone.1 | convolution fusion | flops 806354944 | bytes 5308416 | tf_op jit(solution)/shard_map/while/body/eval_jaxpr/dot_general | solution.py:25
  81.2 0.7 fusion.94
  87.3 8.2 %fusion.89 = (f32[4096,128]{1,0:T(8,128)S(1)}, f32[4096,128]{1,0:T(8,128)S(1)}) fusion(s32[128]{0:T(128)S(1)} %and_select_fusion.8, s32[4096]{0:T(1024)S(1)} %add_select_fusion.4), kind=kLoop, calls=%fused_computation.23.clone.1 | loop fusion | flops 7340032 | bytes 4211200 | tf_op jit(solution)/shard_map/while/body/eval_jaxpr/cos | solution.py:15
  95.5 2.6 %fusion.90 = f32[64,256]{1,0:T(8,128)S(1)} fusion(f32[64,4096]{1,0:T(8,128)S(1)} %get-tuple-element.379, f32[4096,128]{1,0:T(8,128)S(1)} %get-tuple-element.348, f32[4096,128]{1,0:T(8,128)S(1)} %get-tuple-element.349), kind=kOutput, calls=%fused_computation.21.clone.1 | convolution fusion | flops 806354944 | bytes 5308416 | tf_op jit(solution)/shard_map/while/body/eval_jaxpr/dot_general | solution.py:25
  99.5 0.7 fusion.94
  100.9 0.7 fusion.92
  105.6 8.2 %fusion.89 = (f32[4096,128]{1,0:T(8,128)S(1)}, f32[4096,128]{1,0:T(8,128)S(1)}) fusion(s32[128]{0:T(128)S(1)} %and_select_fusion.8, s32[4096]{0:T(1024)S(1)} %add_select_fusion.4), kind=kLoop, calls=%fused_computation.23.clone.1 | loop fusion | flops 7340032 | bytes 4211200 | tf_op jit(solution)/shard_map/while/body/eval_jaxpr/cos | solution.py:15
  113.8 2.6 %fusion.90 = f32[64,256]{1,0:T(8,128)S(1)} fusion(f32[64,4096]{1,0:T(8,128)S(1)} %get-tuple-element.379, f32[4096,128]{1,0:T(8,128)S(1)} %get-tuple-element.348, f32[4096,128]{1,0:T(8,128)S(1)} %get-tuple-element.349), kind=kOutput, calls=%fused_computation.21.clone.1 | convolution fusion | flops 806354944 | bytes 5308416 | tf_op jit(solution)/shard_map/while/body/eval_jaxpr/dot_general | solution.py:25
  117.8 0.7 fusion.94
  123.9 8.2 %fusion.89 = (f32[4096,128]{1,0:T(8,128)S(1)}, f32[4096,128]{1,0:T(8,128)S(1)}) fusion(s32[128]{0:T(128)S(1)} %and_select_fusion.8, s32[4096]{0:T(1024)S(1)} %add_select_fusion.4), kind=kLoop, calls=%fused_computation.23.clone.1 | loop fusion | flops 7340032 | bytes 4211200 | tf_op jit(solution)/shard_map/while/body/eval_jaxpr/cos | solution.py:15
  132.1 2.6 %fusion.90 = f32[64,256]{1,0:T(8,128)S(1)} fusion(f32[64,4096]{1,0:T(8,128)S(1)} %get-tuple-element.379, f32[4096,128]{1,0:T(8,128)S(1)} %get-tuple-element.348, f32[4096,128]{1,0:T(8,128)S(1)} %get-tuple-element.349), kind=kOutput, calls=%fused_computation.21.clone.1 | convolution fusion | flops 806354944 | bytes 5308416 | tf_op jit(solution)/shard_map/while/body/eval_jaxpr/dot_general | solution.py:25
  136.1 0.7 fusion.94
  137.5 0.7 fusion.92
  142.2 8.2 %fusion.89 = (f32[4096,128]{1,0:T(8,128)S(1)}, f32[4096,128]{1,0:T(8,128)S(1)}) fusion(s32[128]{0:T(128)S(1)} %and_select_fusion.8, s32[4096]{0:T(1024)S(1)} %add_select_fusion.4), kind=kLoop, calls=%fused_computation.23.clone.1 | loop fusion | flops 7340032 | bytes 4211200 | tf_op jit(solution)/shard_map/while/body/eval_jaxpr/cos | solution.py:15
  150.4 2.6 %fusion.90 = f32[64,256]{1,0:T(8,128)S(1)} fusion(f32[64,4096]{1,0:T(8,128)S(1)} %get-tuple-element.379, f32[4096,128]{1,0:T(8,128)S(1)} %get-tuple-element.348, f32[4096,128]{1,0:T(8,128)S(1)} %get-tuple-element.349), kind=kOutput, calls=%fused_computation.21.clone.1 | convolution fusion | flops 806354944 | bytes 5308416 | tf_op jit(solution)/shard_map/while/body/eval_jaxpr/dot_general | solution.py:25
  154.4 0.7 fusion.94
  156.5 1.3 copy-done
  157.9 38.1 %reduce-scatter.2.cloned.1.call-done = f32[2,8,2,32,128]{4,3,2,0,1:T(8,128)} async-done(((f32[2,8,2,128,128]{4,3,2,0,1:T(8,128)}), f32[2,8,2,32,128]{4,3,2,0,1:T(8,128)}) %reduce-scatter.2.cloned.1.call-update) | async-done | bytes 524304 | tf_op jit(solution)/shard_map/reduce_scatter | solution.py:52
  195.9 19.9 %all_to_all.5 = f32[2,8,2,32,128]{4,3,2,0,1:T(8,128)S(1)} all-to-all(f32[2,8,2,32,128]{4,3,2,0,1:T(8,128)} %reduce-scatter.2.cloned.1.call-done), channel_id=1, replica_groups=mesh['facet'=8,'slab'=4] {'facet'}, dimensions={1} | all-to-all | bytes 1048576 | tf_op jit(solution)/shard_map/all_to_all | solution.py:53
  (96 shorter events, 41.0 us)
Async XLA Ops:
  6.5 3.5 %copy-start.1 = (s32[8]{0:T(128)S(1)}, s32[8]{0:T(128)}, u32[]{:S(2)}) copy-start(s32[8]{0:T(128)} %param.12) | copy-start | bytes 100
  6.5 189.4 %reduce-scatter.2.cloned.1.call-start = ((), (), s32[]{:S(2)}) async-start(), calls=%async_computation.2 | async-start | bytes 2621440 | tf_op jit(solution)/shard_map/reduce_scatter | solution.py:52
  156.5 1.3 copy-start
Sparse Core Ops, SparseCore 0:
  158.0 37.9 reduce-scatter.1
where the time goes:
time: 224 us; the launch traced here: 223 us
  other arithmetic  82.7 us (37%)
  matrix products  42.3 us (19%)
  waiting for transfers between devices  38.1 us (17%)
  blocking collectives  19.9 us (9%)
  loops' own time  14.2 us (6%)
  between operations  13.4 us (6%)
  local copies, waits for them, and re-layouts  12.8 us (6%)
    cos x8, other arithmetic, phase_pair(): return (jnp.cos(angles), jnp.sin(angles))  65.3 us
    reduce_scatter x1, waiting for transfers between devices, local(): reduced = lax.psum_scatter(summed, 'slab', scatter_dimension=3, tiled=True)  38.1 us
    dot_general x8, matrix products, one_column(): jnp.dot(weighted, tables, precision=highest, preferred_element_type=jnp.f...  20.6 us
    all_to_all x1, blocking collectives, local(): lax.all_to_all(reduced, 'facet', split_axis=1, concat_axis=1, tiled=True)  19.9 us
    another operation x1, loops' own time, facet_terms(): lax.map(one_column, jnp.arange(col_offsets.shape[0], dtype=jnp.int32))  14.2 us
    select_n x16, other arithmetic, phase_pair(): positions[:, None] % GRID * (frequency[..., None, :] % GRID) % GRID  9.97 us
    dot_general x8, matrix products, one_column(): jnp.einsum('qai,aj->qij', row_sin, imag_part, precision=highest)  5.45 us
    dot_general x8, matrix products, one_column(): jnp.einsum('qai,aj->qij', row_sin, real_part, precision=highest)  5.44 us
  transfers between devices with their start and end apart: 1, of which 1 were waited for; matrix products, arithmetic and copies ran while one was open for 0% of the time, Pallas kernels for 0%

commit v1 on v0

v1 whole, which is shorter than its diff:
```python
import functools
import math

import jax
import jax.numpy as jnp
from jax import lax
from jax.experimental import pallas as pl
from jax.experimental.pallas import tpu as pltpu
from jax.sharding import PartitionSpec as P

GRID = 32768
CONTRIB = 128
HALF = 256
TURN = 2 * GRID
MESH = pl.DeviceIdType.MESH
F32 = jnp.float32
BF16 = jnp.bfloat16


def cos_sin(steps):
    steps = steps & (TURN - 1)
    quadrant = (steps + TURN // 8) >> 14
    x = (steps - (quadrant << 14)).astype(F32) * (2.0 * math.pi / TURN)
    y = x * x
    s = x + x * y * (-1 / 6 + y * (1 / 120 + y * (-1 / 5040 + y * (1 / 362880))))
    c = 1.0 + y * (-0.5 + y * (1 / 24 + y * (-1 / 720 + y * (1 / 40320))))
    odd = (quadrant & 1) == 1
    cos = jnp.where(odd, s, c)
    sin = jnp.where(odd, c, s)
    cos = jnp.where(((quadrant + 1) & 2) == 2, -cos, cos)
    sin = jnp.where((quadrant & 2) == 2, -sin, sin)
    return cos, sin


def split(x):
    high = x.astype(BF16)
    return high, (x - high.astype(F32)).astype(BF16)


def dot(a, b):
    return jnp.dot(a, b, preferred_element_type=F32)


def kernel(
    groups, slabs, scale,
    facet_ref, row_taper_ref, col_taper_ref, offset_ref, own_offset_ref, col_ref, row_ref,
    out_ref,
    even, odd, outgoing, incoming, offsets, part_out, part_in,
    off_send, off_recv, send, recv, part_send, part_recv,
):
    me = lax.axis_index("facet")
    slab = lax.axis_index("slab")
    rows, width = facet_ref.shape[1], facet_ref.shape[2]
    blocks = width // (2 * HALF)
    subs = row_ref.shape[1]
    pairs = groups // 2
    my_pair = me // 2
    keep = CONTRIB // slabs

    barrier = pltpu.get_barrier_semaphore()
    for d in range(1, groups):
        pl.semaphore_signal(barrier, inc=1, device_id={"facet": lax.rem(me + d, groups)}, device_id_type=MESH)
    for d in range(1, slabs):
        pl.semaphore_signal(barrier, inc=1, device_id={"slab": lax.rem(slab + d, slabs)}, device_id_type=MESH)

    mirror = (
        lax.broadcasted_iota(jnp.int32, (HALF, HALF), 0) + lax.broadcasted_iota(jnp.int32, (HALF, HALF), 1) == HALF - 1
    ).astype(F32).astype(BF16)
    for j in range(blocks):
        lo, mid, hi = 2 * HALF * j, 2 * HALF * j + HALF, 2 * HALF * (j + 1)
        left = facet_ref[0, :, lo:mid] * col_taper_ref[:, lo:mid]
        right = facet_ref[0, :, mid:hi] * col_taper_ref[:, mid:hi]
        left_high, left_low = split(left)
        turned = dot(left_high, mirror) + dot(left_low, mirror)
        band = slice(j * rows, (j + 1) * rows)
        for ref, value in ((even, right + turned), (odd, right - turned)):
            high, low = split(value)
            ref[band, :HALF] = high
            ref[band, HALF : 2 * HALF] = high
            ref[band, 2 * HALF :] = low

    pl.semaphore_wait(barrier, groups - 1 + slabs - 1)

    def offset_copy(peer, home):
        return pltpu.make_async_remote_copy(
            src_ref=offset_ref, dst_ref=offsets.at[home], send_sem=off_send.at[peer], recv_sem=off_recv.at[home],
            device_id={"facet": peer}, device_id_type=MESH,
        )

    def block_copy(peer, home):
        return pltpu.make_async_remote_copy(
            src_ref=outgoing.at[peer], dst_ref=incoming.at[home], send_sem=send.at[peer], recv_sem=recv.at[home],
            device_id={"facet": peer}, device_id_type=MESH,
        )

    def part_copy(peer, home):
        return pltpu.make_async_remote_copy(
            src_ref=part_out.at[peer], dst_ref=part_in.at[home], send_sem=part_send.at[peer], recv_sem=part_recv.at[home],
            device_id={"slab": peer}, device_id_type=MESH,
        )

    for d in range(1, groups):
        offset_copy(lax.rem(me + d, groups), me).start()
    offsets[me] = offset_ref[...]

    order = sorted(range(pairs), key=lambda d: -min(d, pairs - d))
    lane = lax.broadcasted_iota(jnp.int32, (1, 2 * CONTRIB), 1)
    second = lane >= CONTRIB
    twice = 2 * lax.broadcasted_iota(jnp.int32, (HALF, 1), 0) + 1
    centre = 2 * own_offset_ref[0, 1] + 2 * HALF - 1 + 4 * HALF * lax.broadcasted_iota(jnp.int32, (blocks, 1), 0)
    for d in order:
        pair = lax.rem(my_pair + d, pairs)
        frequency = (lane & (CONTRIB - 1)) + jnp.where(second, col_ref[2 * pair + 1], col_ref[2 * pair])
        cos, sin = cos_sin(twice * frequency)
        turn_cos, turn_sin = cos_sin(centre * frequency)
        cos_high, cos_low = split(cos)
        sin_high, sin_low = split(sin)
        evens = dot(even[...], jnp.concatenate([cos_high, cos_low, cos_high], axis=0))
        odds = dot(odd[...], jnp.concatenate([sin_high, sin_low, sin_high], axis=0))
        real = jnp.zeros((rows, 2 * CONTRIB), F32)
        imag = jnp.zeros((rows, 2 * CONTRIB), F32)
        for j in range(blocks):
            e = evens[j * rows : (j + 1) * rows]
            o = odds[j * rows : (j + 1) * rows]
            tc, ts = turn_cos[j : j + 1], turn_sin[j : j + 1]
            real = real + (tc * e - ts * o)
            imag = imag - (ts * e + tc * o)
        for side in range(2):
            span = slice(side * CONTRIB, (side + 1) * CONTRIB)
            outgoing[2 * pair + side, 0] = real[:, span]
            outgoing[2 * pair + side, 1] = imag[:, span]
        if d:
            block_copy(2 * pair, me).start()
            block_copy(2 * pair + 1, me).start()
    twin = me + 1 - 2 * lax.rem(me, 2)
    block_copy(twin, me).start()
    incoming[me] = outgoing[me]

    for d in range(1, groups):
        peer = lax.rem(me + d, groups)
        offset_copy(peer, peer).wait_recv()

    sub = lax.broadcasted_iota(jnp.int32, (subs * CONTRIB, 1), 0)
    row_frequency = sub
    for q in range(subs):
        row_frequency = jnp.where(sub // CONTRIB == q, sub - q * CONTRIB + row_ref[me, q], row_frequency)
    spot = lax.broadcasted_iota(jnp.int32, (1, 2 * rows), 1)
    taper = jnp.concatenate([row_taper_ref[...], row_taper_ref[...]], axis=1)
    tables = []
    for d in order:
        pair = lax.rem(my_pair + pairs - d, pairs)
        base = jnp.where(spot < rows, offsets[2 * pair, :, 0:1], offsets[2 * pair + 1, :, 0:1])
        place = base + jnp.where(spot < rows, spot, spot - rows) + slab * rows
        cos, sin = cos_sin(2 * row_frequency * place)
        high, low = split(jnp.concatenate([cos * taper, sin * taper], axis=1))
        tables.append(jnp.concatenate([high, high, low], axis=1))
    total = None
    for d, table in zip(order, tables):
        pair = lax.rem(my_pair + pairs - d, pairs)
        for side in range(2):
            peer = 2 * pair + side
            if d:
                block_copy(peer, peer).wait_recv()
        if not d:
            block_copy(twin, twin).wait_recv()
        real = incoming[pl.ds(2 * pair, 2), 0].reshape(2 * rows, CONTRIB)
        imag = incoming[pl.ds(2 * pair, 2), 1].reshape(2 * rows, CONTRIB)
        high, low = split(
            jnp.concatenate(
                [jnp.concatenate([real, imag], axis=1), jnp.concatenate([imag, -real], axis=1)], axis=0
            )
        )
        term = dot(table, jnp.concatenate([high, low, high], axis=0))
        total = term if total is None else total + term

    for t in range(slabs):
        for q in range(subs):
            start = q * CONTRIB + t * keep
            part_out[t, q] = total[start : start + keep]
    for d in range(1, slabs):
        part_copy(lax.rem(slab + d, slabs), slab).start()
    result = part_out[slab]
    for d in range(1, slabs):
        peer = lax.rem(slab + d, slabs)
        part_copy(peer, peer).wait_recv()
        result = result + part_in[peer]
    result = result * scale
    out_ref[0, 0] = result[:, :, :CONTRIB]
    out_ref[1, 0] = result[:, :, CONTRIB:]

    for d in range(1, groups):
        peer = lax.rem(me + d, groups)
        offset_copy(peer, me).wait_send()
        block_copy(peer, me).wait_send()
    for d in range(1, slabs):
        part_copy(lax.rem(slab + d, slabs), slab).wait_send()


def solution(mesh):
    groups, slabs = mesh.shape["facet"], mesh.shape["slab"]

    def local(facets, row_taper, col_taper, facet_offsets, col_offsets, row_offsets):
        rows, width = facets.shape[1], facets.shape[2]
        subs = row_offsets.shape[1]
        keep = CONTRIB // slabs
        stacked = width // (2 * HALF) * rows
        scale = 1.0 / math.sqrt(facets.shape[0] * groups * rows * slabs * width)
        vmem = pl.BlockSpec(memory_space=pltpu.VMEM)
        smem = pl.BlockSpec(memory_space=pltpu.SMEM)
        dma = pltpu.SemaphoreType.DMA
        return pl.pallas_call(
            functools.partial(kernel, groups, slabs, scale),
            out_shape=jax.ShapeDtypeStruct((2, 1, subs, keep, CONTRIB), F32),
            in_specs=[vmem, vmem, vmem, vmem, smem, smem, smem],
            out_specs=vmem,
            scratch_shapes=[
                pltpu.VMEM((stacked, 3 * HALF), BF16),
                pltpu.VMEM((stacked, 3 * HALF), BF16),
                pltpu.VMEM((groups, 2, rows, CONTRIB), F32),
                pltpu.VMEM((groups, 2, rows, CONTRIB), F32),
                pltpu.VMEM((groups, 1, 2), jnp.int32),
                pltpu.VMEM((slabs, subs, keep, 2 * CONTRIB), F32),
                pltpu.VMEM((slabs, subs, keep, 2 * CONTRIB), F32),
                dma((groups,)), dma((groups,)), dma((groups,)), dma((groups,)), dma((slabs,)), dma((slabs,)),
            ],
            compiler_params=pltpu.CompilerParams(collective_id=0, has_side_effects=True),
        )(facets, row_taper.reshape(1, rows), col_taper.reshape(1, width), facet_offsets, facet_offsets, col_offsets, row_offsets)

    placed = (P("facet", "slab", None), P("slab"), P(), P("facet", None), P(), P())
    return jax.shard_map(
        local, mesh=mesh, in_specs=placed, out_specs=P(None, "facet", None, "slab", None), check_vma=False
    )
```

time: 224 us -> 28.4 us (0.13)
  other arithmetic: 82.7 us -> 0 us
  matrix products: 42.3 us -> 0 us
  waiting for transfers between devices: 38.1 us -> 0 us
  Pallas kernels: 0 us -> 25.4 us
  blocking collectives: 19.9 us -> 0 us
  loops' own time: 14.2 us -> 0 us
  between operations: 13.4 us -> 0.01 us
  local copies, waits for them, and re-layouts: 12.8 us -> 2.82 us
    cos x8 -> x0, other arithmetic: 65.3 us -> none  [phase_pair(): return (jnp.cos(angles), jnp.sin(angles))]
    dot_general x40 -> x0, matrix products: 42.3 us -> none  [the longest x8 20.6 us: one_column(): jnp.dot(weighted, tables, precision=highest, preferred_element_type=jnp.f...]
    reduce_scatter x1 -> x0, waiting for transfers between devices: 38.1 us -> none  [local(): reduced = lax.psum_scatter(summed, 'slab', scatter_dimension=3, tiled=True)]
    pallas_call x0 -> x1, Pallas kernels: none -> 25.4 us  [local(): pl.pallas_call(functools.partial(kernel, groups, slabs, scale), out_shape...]
    all_to_all x1 -> x0, blocking collectives: 19.9 us -> none  [local(): lax.all_to_all(reduced, 'facet', split_axis=1, concat_axis=1, tiled=True)]
    select_n x32 -> x0, other arithmetic: 15.1 us -> none  [the longest x16 9.97 us: phase_pair(): positions[:, None] % GRID * (frequency[..., None, :] % GRID) % GRID]
    another operation x1 -> x0, loops' own time: 14.2 us -> none  [facet_terms(): lax.map(one_column, jnp.arange(col_offsets.shape[0], dtype=jnp.int32))]
    dynamic_slice x16 -> x0, local copies, waits for them, and re-layouts: 9.28 us -> none  [the longest x8 4.64 us: one_column(): col_cos, col_sin = phase_pair(col_pos, frequency + col_offsets[column])]
  transfers between devices with their start and end apart: 1 -> 0, of which waited for: 1 -> 0; matrix products, arithmetic and copies ran while one was open for 0% -> 0% of each run, Pallas kernels for 0% -> 0%
where the time goes in v1:
time: 28.4 us; the launch traced here: 28.2 us
  Pallas kernels  25.4 us (89%)
  local copies, waits for them, and re-layouts  2.82 us (10%)
    pallas_call x1, Pallas kernels, local(): pl.pallas_call(functools.partial(kernel, groups, slabs, scale), out_shape...  25.4 us
    unnamed x4, local copies, waits for them, and re-layouts  2.82 us

profile of v1, /device:TPU:0, one launch (start us, length us, event | category | flops | bytes accessed | tf_op | source)
XLA Modules:
  0.0 28.2 jit_solution(10207604928314673184)
XLA Ops:
  0.0 0.0 copy-start
  0.0 0.7 %copy-done = s32[8,2]{0,1:T(2,128)S(1)} copy-done((s32[8,2]{0,1:T(2,128)S(1)}, s32[8,2]{0,1:T(2,128)}, u32[]{:S(2)}) %copy-start) | copy-done | bytes 88
  0.7 0.7 %copy.7.row_ref = s32[8,2]{1,0:T(8,128)} copy(s32[8,2]{0,1:T(2,128)S(1)} %copy-done) | data formatting | bytes 128 | tf_op args[5]
  1.4 25.4 %shard_map.64 = f32[2,1,2,32,128]{4,3,2,1,0:T(8,128)} custom-call(f32[1,64,4096]{2,1,0:T(8,128)} %facet_ref.1, f32[1,64]{1,0:T(1,128)} %bitcast.3, f32[1,4096]{1,0:T(1,128)} %bitcast.2, s32[1,2]{1,0:T(1,128)} %own_offset_ref.1, s32[1,2]{1,0:T(1,128)} %own_offset_ref.1, s32[8]{0:T(128)} %col_ref.1, s32[8,2]{1,0:T(8,128)} %copy.7.row_ref), custom_call_target="tpu_custom_call" | custom-call | tf_op jit(solution)/shard_map/pallas_call | solution.py:211
  26.8 1.5 %copy.9 = f32[2,1,2,32,128]{4,3,2,1,0:T(8,128)} copy(f32[2,1,2,32,128]{4,3,2,1,0:T(8,128)} %shard_map.64) | data formatting | bytes 131072
Async XLA Ops:
  0.0 0.7 %copy-start = (s32[8,2]{0,1:T(2,128)S(1)}, s32[8,2]{0,1:T(2,128)}, u32[]{:S(2)}) copy-start(s32[8,2]{0,1:T(2,128)} %param.11) | copy-start | bytes 196

commit v2 on v1

v2 whole, which is shorter than its diff:
```python
import functools
import math

import jax
import jax.numpy as jnp
from jax import lax
from jax.experimental import pallas as pl
from jax.experimental.pallas import tpu as pltpu
from jax.sharding import PartitionSpec as P

GRID = 32768
CONTRIB = 128
HALF = 256
TURN = 2 * GRID
MESH = pl.DeviceIdType.MESH
F32 = jnp.float32
BF16 = jnp.bfloat16


def cos_sin(steps):
    steps = steps & (TURN - 1)
    quadrant = (steps + TURN // 8) >> 14
    x = (steps - (quadrant << 14)).astype(F32) * (2.0 * math.pi / TURN)
    y = x * x
    s = x + x * y * (-1 / 6 + y * (1 / 120 + y * (-1 / 5040 + y * (1 / 362880))))
    c = 1.0 + y * (-0.5 + y * (1 / 24 + y * (-1 / 720 + y * (1 / 40320))))
    odd = (quadrant & 1) == 1
    cos = jnp.where(odd, s, c)
    sin = jnp.where(odd, c, s)
    cos = jnp.where(((quadrant + 1) & 2) == 2, -cos, cos)
    sin = jnp.where((quadrant & 2) == 2, -sin, sin)
    return cos, sin


def split(x):
    high = x.astype(BF16)
    return high, (x - high.astype(F32)).astype(BF16)


def dot(a, b):
    return jnp.dot(a, b, preferred_element_type=F32)


def kernel(
    groups, slabs, scale,
    facet_ref, row_taper_ref, col_taper_ref, offset_ref, own_offset_ref, col_ref, row_ref,
    out_ref,
    even, odd, outgoing, incoming, offsets, part_out, part_in, cross_out, cross_in,
    off_send, off_recv, send, recv, part_send, part_recv, cross_send, cross_recv,
):
    me = lax.axis_index("facet")
    slab = lax.axis_index("slab")
    rows, width = facet_ref.shape[1], facet_ref.shape[2]
    blocks = width // (2 * HALF)
    subs = row_ref.shape[0]
    half = groups // 2
    half_pairs = half // 2
    mine = lax.rem(me, half)
    base = me - mine
    other_base = half - base
    partner = other_base + mine
    my_pair = mine // 2
    keep = CONTRIB // slabs

    barrier = pltpu.get_barrier_semaphore()
    for d in range(1, half):
        pl.semaphore_signal(
            barrier, inc=1, device_id={"facet": base + lax.rem(mine + d, half)}, device_id_type=MESH
        )
    for d in range(1, slabs):
        pl.semaphore_signal(barrier, inc=1, device_id={"slab": lax.rem(slab + d, slabs)}, device_id_type=MESH)
    pl.semaphore_signal(barrier, inc=1, device_id={"facet": partner}, device_id_type=MESH)

    mirror = (
        lax.broadcasted_iota(jnp.int32, (HALF, HALF), 0) + lax.broadcasted_iota(jnp.int32, (HALF, HALF), 1) == HALF - 1
    ).astype(F32).astype(BF16)
    for j in range(blocks):
        lo, mid, hi = 2 * HALF * j, 2 * HALF * j + HALF, 2 * HALF * (j + 1)
        left = facet_ref[0, :, lo:mid] * col_taper_ref[:, lo:mid]
        right = facet_ref[0, :, mid:hi] * col_taper_ref[:, mid:hi]
        left_high, left_low = split(left)
        turned = dot(left_high, mirror) + dot(left_low, mirror)
        band = slice(j * rows, (j + 1) * rows)
        for ref, value in ((even, right + turned), (odd, right - turned)):
            high, low = split(value)
            ref[band, :HALF] = high
            ref[band, HALF : 2 * HALF] = high
            ref[band, 2 * HALF :] = low

    pl.semaphore_wait(barrier, half - 1 + slabs - 1 + 1)

    def offset_copy(peer, home):
        return pltpu.make_async_remote_copy(
            src_ref=offset_ref, dst_ref=offsets.at[home], send_sem=off_send.at[peer], recv_sem=off_recv.at[home],
            device_id={"facet": base + peer}, device_id_type=MESH,
        )

    def block_copy(kind, peer, home):
        return pltpu.make_async_remote_copy(
            src_ref=outgoing.at[kind, peer], dst_ref=incoming.at[kind, home],
            send_sem=send.at[kind, peer], recv_sem=recv.at[kind, home],
            device_id={"facet": base + peer}, device_id_type=MESH,
        )

    def part_copy(kind, peer, home):
        return pltpu.make_async_remote_copy(
            src_ref=part_out.at[kind, peer], dst_ref=part_in.at[kind, home],
            send_sem=part_send.at[kind, peer], recv_sem=part_recv.at[kind, home],
            device_id={"slab": peer}, device_id_type=MESH,
        )

    cross_copy = pltpu.make_async_remote_copy(
        src_ref=cross_out, dst_ref=cross_in, send_sem=cross_send, recv_sem=cross_recv,
        device_id={"facet": partner}, device_id_type=MESH,
    )

    for d in range(1, half):
        offset_copy(lax.rem(mine + d, half), mine).start()
    offsets[mine] = offset_ref[...]

    order = sorted(range(half_pairs), key=lambda d: -min(d, half_pairs - d))
    twin = mine + 1 - 2 * lax.rem(mine, 2)
    lane = lax.broadcasted_iota(jnp.int32, (1, 2 * CONTRIB), 1)
    second = lane >= CONTRIB
    twice = 2 * lax.broadcasted_iota(jnp.int32, (HALF, 1), 0) + 1
    centre = 2 * own_offset_ref[0, 1] + 2 * HALF - 1 + 4 * HALF * lax.broadcasted_iota(jnp.int32, (blocks, 1), 0)
    for kind, first in ((0, other_base), (1, base)):
        for d in order:
            pair = lax.rem(my_pair + d, half_pairs)
            column = first + 2 * pair
            frequency = (lane & (CONTRIB - 1)) + jnp.where(second, col_ref[column + 1], col_ref[column])
            cos, sin = cos_sin(twice * frequency)
            turn_cos, turn_sin = cos_sin(centre * frequency)
            cos_high, cos_low = split(cos)
            sin_high, sin_low = split(sin)
            evens = dot(even[...], jnp.concatenate([cos_high, cos_low, cos_high], axis=0))
            odds = dot(odd[...], jnp.concatenate([sin_high, sin_low, sin_high], axis=0))
            real = jnp.zeros((rows, 2 * CONTRIB), F32)
            imag = jnp.zeros((rows, 2 * CONTRIB), F32)
            for j in range(blocks):
                e = evens[j * rows : (j + 1) * rows]
                o = odds[j * rows : (j + 1) * rows]
                tc, ts = turn_cos[j : j + 1], turn_sin[j : j + 1]
                real = real + (tc * e - ts * o)
                imag = imag - (ts * e + tc * o)
            for side in range(2):
                span = slice(side * CONTRIB, (side + 1) * CONTRIB)
                outgoing[kind, 2 * pair + side, 0] = real[:, span]
                outgoing[kind, 2 * pair + side, 1] = imag[:, span]
            if d:
                block_copy(kind, 2 * pair, mine).start()
                block_copy(kind, 2 * pair + 1, mine).start()
        block_copy(kind, twin, mine).start()
        incoming[kind, mine] = outgoing[kind, mine]

    for d in range(1, half):
        peer = lax.rem(mine + d, half)
        offset_copy(peer, peer).wait_recv()

    sub = lax.broadcasted_iota(jnp.int32, (subs * CONTRIB, 1), 0)
    spot = lax.broadcasted_iota(jnp.int32, (1, 2 * rows), 1)
    taper = jnp.concatenate([row_taper_ref[...], row_taper_ref[...]], axis=1)
    for kind, column in ((0, partner), (1, me)):
        row_frequency = sub
        for q in range(subs):
            row_frequency = jnp.where(sub // CONTRIB == q, sub - q * CONTRIB + row_ref[q, column], row_frequency)
        total = None
        for d in order:
            pair = lax.rem(my_pair + half_pairs - d, half_pairs)
            start = jnp.where(spot < rows, offsets[2 * pair, :, 0:1], offsets[2 * pair + 1, :, 0:1])
            place = start + jnp.where(spot < rows, spot, spot - rows) + slab * rows
            cos, sin = cos_sin(2 * row_frequency * place)
            high, low = split(jnp.concatenate([cos * taper, sin * taper], axis=1))
            table = jnp.concatenate([high, high, low], axis=1)
            if d:
                block_copy(kind, 2 * pair, 2 * pair).wait_recv()
                block_copy(kind, 2 * pair + 1, 2 * pair + 1).wait_recv()
            else:
                block_copy(kind, twin, twin).wait_recv()
            real = incoming[kind, pl.ds(2 * pair, 2), 0].reshape(2 * rows, CONTRIB)
            imag = incoming[kind, pl.ds(2 * pair, 2), 1].reshape(2 * rows, CONTRIB)
            high, low = split(
                jnp.concatenate(
                    [jnp.concatenate([real, imag], axis=1), jnp.concatenate([imag, -real], axis=1)], axis=0
                )
            )
            term = dot(table, jnp.concatenate([high, low, high], axis=0))
            total = term if total is None else total + term
        for t in range(slabs):
            for q in range(subs):
                start = q * CONTRIB + t * keep
                part_out[kind, t, q] = total[start : start + keep]
        for d in range(1, slabs):
            part_copy(kind, lax.rem(slab + d, slabs), slab).start()

    def summed(kind):
        result = part_out[kind, slab]
        for d in range(1, slabs):
            peer = lax.rem(slab + d, slabs)
            part_copy(kind, peer, peer).wait_recv()
            result = result + part_in[kind, peer]
        return result

    cross_out[...] = summed(0)
    cross_copy.start()
    result = summed(1)
    cross_copy.wait_recv()
    result = (result + cross_in[...]) * scale
    out_ref[0, 0] = result[:, :, :CONTRIB]
    out_ref[1, 0] = result[:, :, CONTRIB:]

    for d in range(1, half):
        peer = lax.rem(mine + d, half)
        offset_copy(peer, mine).wait_send()
        for kind in range(2):
            block_copy(kind, peer, mine).wait_send()
    for kind in range(2):
        for d in range(1, slabs):
            part_copy(kind, lax.rem(slab + d, slabs), slab).wait_send()
    cross_copy.wait_send()


def solution(mesh):
    groups, slabs = mesh.shape["facet"], mesh.shape["slab"]

    def local(facets, row_taper, col_taper, facet_offsets, col_offsets, row_offsets):
        rows, width = facets.shape[1], facets.shape[2]
        subs = row_offsets.shape[1]
        keep = CONTRIB // slabs
        half = groups // 2
        stacked = width // (2 * HALF) * rows
        scale = 1.0 / math.sqrt(facets.shape[0] * groups * rows * slabs * width)
        vmem = pl.BlockSpec(memory_space=pltpu.VMEM)
        smem = pl.BlockSpec(memory_space=pltpu.SMEM)
        dma = pltpu.SemaphoreType.DMA
        return pl.pallas_call(
            functools.partial(kernel, groups, slabs, scale),
            out_shape=jax.ShapeDtypeStruct((2, 1, subs, keep, CONTRIB), F32),
            in_specs=[vmem, vmem, vmem, vmem, smem, smem, smem],
            out_specs=vmem,
            scratch_shapes=[
                pltpu.VMEM((stacked, 3 * HALF), BF16),
                pltpu.VMEM((stacked, 3 * HALF), BF16),
                pltpu.VMEM((2, half, 2, rows, CONTRIB), F32),
                pltpu.VMEM((2, half, 2, rows, CONTRIB), F32),
                pltpu.VMEM((half, 1, 2), jnp.int32),
                pltpu.VMEM((2, slabs, subs, keep, 2 * CONTRIB), F32),
                pltpu.VMEM((2, slabs, subs, keep, 2 * CONTRIB), F32),
                pltpu.VMEM((subs, keep, 2 * CONTRIB), F32),
                pltpu.VMEM((subs, keep, 2 * CONTRIB), F32),
                dma((half,)), dma((half,)), dma((2, half)), dma((2, half)), dma((2, slabs)), dma((2, slabs)), dma, dma,
            ],
            compiler_params=pltpu.CompilerParams(collective_id=0, has_side_effects=True),
        )(facets, row_taper.reshape(1, rows), col_taper.reshape(1, width), facet_offsets, facet_offsets, col_offsets, row_offsets.T)

    placed = (P("facet", "slab", None), P("slab"), P(), P("facet", None), P(), P())
    return jax.shard_map(
        local, mesh=mesh, in_specs=placed, out_specs=P(None, "facet", None, "slab", None), check_vma=False
    )
```

time: 28.4 us -> 25.2 us (0.89)
  Pallas kernels: 25.4 us -> 23.5 us
  local copies, waits for them, and re-layouts: 2.82 us -> 1.47 us
    pallas_call x1, Pallas kernels: 25.4 us -> 23.5 us  [local(): pl.pallas_call(functools.partial(kernel, groups, slabs, scale), out_shape...]
    unnamed x4 -> x1, local copies, waits for them, and re-layouts: 2.82 us -> 1.47 us
where the time goes in v2:
time: 25.2 us; the launch traced here: 25 us
  Pallas kernels  23.5 us (93%)
  local copies, waits for them, and re-layouts  1.47 us (6%)
    pallas_call x1, Pallas kernels, local(): pl.pallas_call(functools.partial(kernel, groups, slabs, scale), out_shape...  23.5 us
    unnamed x1, local copies, waits for them, and re-layouts  1.47 us

profile of v2, /device:TPU:0, one launch (start us, length us, event | category | flops | bytes accessed | tf_op | source)
XLA Modules:
  0.0 25.0 jit_solution(3329158940597448987)
XLA Ops:
  0.0 23.5 %shard_map.64 = f32[2,1,2,32,128]{4,3,2,1,0:T(8,128)} custom-call(f32[1,64,4096]{2,1,0:T(8,128)} %facet_ref.1, f32[1,64]{1,0:T(1,128)} %bitcast.5, f32[1,4096]{1,0:T(1,128)} %bitcast.3, s32[1,2]{1,0:T(1,128)} %own_offset_ref.1, s32[1,2]{1,0:T(1,128)} %own_offset_ref.1, s32[8]{0:T(128)} %col_ref.1, s32[2,8]{1,0:T(2,128)} %bitcast.4), custom_call_target="tpu_custom_call" | custom-call | tf_op jit(solution)/shard_map/pallas_call | solution.py:236
  23.5 1.5 %copy.8 = f32[2,1,2,32,128]{4,3,2,1,0:T(8,128)} copy(f32[2,1,2,32,128]{4,3,2,1,0:T(8,128)} %shard_map.64) | data formatting | bytes 131072

commit v3 on v2

v3 whole, which is shorter than its diff:
```python
import functools
import math

import jax
import jax.numpy as jnp
from jax import lax
from jax.experimental import pallas as pl
from jax.experimental.pallas import tpu as pltpu
from jax.sharding import PartitionSpec as P

GRID = 32768
CONTRIB = 128
HALF = 256
TURN = 2 * GRID
CHUNKS = 4
PIECES = 2
MESH = pl.DeviceIdType.MESH
F32 = jnp.float32
BF16 = jnp.bfloat16


def cos_sin(steps):
    steps = steps & (TURN - 1)
    quadrant = (steps + TURN // 8) >> 14
    x = (steps - (quadrant << 14)).astype(F32) * (2.0 * math.pi / TURN)
    y = x * x
    s = x + x * y * (-1 / 6 + y * (1 / 120 + y * (-1 / 5040 + y * (1 / 362880))))
    c = 1.0 + y * (-0.5 + y * (1 / 24 + y * (-1 / 720 + y * (1 / 40320))))
    odd = (quadrant & 1) == 1
    cos = jnp.where(odd, s, c)
    sin = jnp.where(odd, c, s)
    cos = jnp.where(((quadrant + 1) & 2) == 2, -cos, cos)
    sin = jnp.where((quadrant & 2) == 2, -sin, sin)
    return cos, sin


def split(x):
    high = x.astype(BF16)
    return high, (x - high.astype(F32)).astype(BF16)


def dot(a, b):
    return jnp.dot(a, b, preferred_element_type=F32)


def kernel(
    groups, slabs, scale,
    facet_ref, row_taper_ref, col_taper_ref, offset_ref, own_offset_ref, col_ref, row_ref,
    out_ref,
    facet_buf, out_buf, even, odd, outgoing, incoming, offsets, part_out, part_in, cross_out, cross_in,
    load, store, off_send, off_recv, send, recv, part_send, part_recv, cross_send, cross_recv,
):
    me = lax.axis_index("facet")
    slab = lax.axis_index("slab")
    rows, width = facet_ref.shape[1], facet_ref.shape[2]
    blocks = width // (2 * HALF)
    subs = row_ref.shape[0]
    half = groups // 2
    half_pairs = half // 2
    mine = lax.rem(me, half)
    base = me - mine
    other_base = half - base
    partner = other_base + mine
    my_pair = mine // 2
    keep = CONTRIB // slabs
    share = keep // PIECES
    chunk = width // CHUNKS

    def facet_copy(n):
        span = slice(n * chunk, (n + 1) * chunk)
        return pltpu.make_async_copy(facet_ref.at[0, :, span], facet_buf.at[:, span], load.at[n])

    for n in range(CHUNKS):
        facet_copy(n).start()

    barrier = pltpu.get_barrier_semaphore()
    for d in range(1, half):
        pl.semaphore_signal(
            barrier, inc=1, device_id={"facet": base + lax.rem(mine + d, half)}, device_id_type=MESH
        )
    for d in range(1, slabs):
        pl.semaphore_signal(barrier, inc=1, device_id={"slab": lax.rem(slab + d, slabs)}, device_id_type=MESH)
    pl.semaphore_signal(barrier, inc=1, device_id={"facet": partner}, device_id_type=MESH)

    order = sorted(range(half_pairs), key=lambda d: -min(d, half_pairs - d))
    lane = lax.broadcasted_iota(jnp.int32, (1, 2 * CONTRIB), 1)
    second = lane >= CONTRIB
    twice = 2 * lax.broadcasted_iota(jnp.int32, (HALF, 1), 0) + 1
    centre = 2 * own_offset_ref[0, 1] + 2 * HALF - 1 + 4 * HALF * lax.broadcasted_iota(jnp.int32, (blocks, 1), 0)

    def column_tables(column):
        frequency = (lane & (CONTRIB - 1)) + jnp.where(second, col_ref[column + 1], col_ref[column])
        cos, sin = cos_sin(twice * frequency)
        cos_high, cos_low = split(cos)
        sin_high, sin_low = split(sin)
        return (
            jnp.concatenate([cos_high, cos_low, cos_high], axis=0),
            jnp.concatenate([sin_high, sin_low, sin_high], axis=0),
        ) + cos_sin(centre * frequency)

    tables = column_tables(other_base + 2 * lax.rem(my_pair + order[0], half_pairs))

    mirror = (
        lax.broadcasted_iota(jnp.int32, (HALF, HALF), 0) + lax.broadcasted_iota(jnp.int32, (HALF, HALF), 1) == HALF - 1
    ).astype(F32).astype(BF16)
    for j in range(blocks):
        if j % (blocks // CHUNKS) == 0:
            facet_copy(j // (blocks // CHUNKS)).wait()
        lo, mid, hi = 2 * HALF * j, 2 * HALF * j + HALF, 2 * HALF * (j + 1)
        left = facet_buf[:, lo:mid] * col_taper_ref[:, lo:mid]
        right = facet_buf[:, mid:hi] * col_taper_ref[:, mid:hi]
        left_high, left_low = split(left)
        turned = dot(left_high, mirror) + dot(left_low, mirror)
        band = slice(j * rows, (j + 1) * rows)
        for ref, value in ((even, right + turned), (odd, right - turned)):
            high, low = split(value)
            ref[band, :HALF] = high
            ref[band, HALF : 2 * HALF] = high
            ref[band, 2 * HALF :] = low

    pl.semaphore_wait(barrier, half - 1 + slabs - 1 + 1)

    def offset_copy(peer, home):
        return pltpu.make_async_remote_copy(
            src_ref=offset_ref, dst_ref=offsets.at[home], send_sem=off_send.at[peer], recv_sem=off_recv.at[home],
            device_id={"facet": base + peer}, device_id_type=MESH,
        )

    def block_copy(kind, peer, home):
        return pltpu.make_async_remote_copy(
            src_ref=outgoing.at[kind, peer], dst_ref=incoming.at[kind, home],
            send_sem=send.at[kind, peer], recv_sem=recv.at[kind, home],
            device_id={"facet": base + peer}, device_id_type=MESH,
        )

    def part_copy(kind, piece, peer, home):
        return pltpu.make_async_remote_copy(
            src_ref=part_out.at[kind, peer, piece], dst_ref=part_in.at[kind, home, piece],
            send_sem=part_send.at[kind, peer, piece], recv_sem=part_recv.at[kind, home, piece],
            device_id={"slab": peer}, device_id_type=MESH,
        )

    def cross_copy(piece):
        return pltpu.make_async_remote_copy(
            src_ref=cross_out.at[piece], dst_ref=cross_in.at[piece],
            send_sem=cross_send.at[piece], recv_sem=cross_recv.at[piece],
            device_id={"facet": partner}, device_id_type=MESH,
        )

    for d in range(1, half):
        offset_copy(lax.rem(mine + d, half), mine).start()
    offsets[mine] = offset_ref[...]

    twin = mine + 1 - 2 * lax.rem(mine, 2)
    for kind, first in ((0, other_base), (1, base)):
        for d in order:
            pair = lax.rem(my_pair + d, half_pairs)
            column = first + 2 * pair
            if tables is None:
                tables = column_tables(column)
            cos_table, sin_table, turn_cos, turn_sin = tables
            tables = None
            evens = dot(even[...], cos_table)
            odds = dot(odd[...], sin_table)
            real = jnp.zeros((rows, 2 * CONTRIB), F32)
            imag = jnp.zeros((rows, 2 * CONTRIB), F32)
            for j in range(blocks):
                e = evens[j * rows : (j + 1) * rows]
                o = odds[j * rows : (j + 1) * rows]
                tc, ts = turn_cos[j : j + 1], turn_sin[j : j + 1]
                real = real + (tc * e - ts * o)
                imag = imag - (ts * e + tc * o)
            for side in range(2):
                span = slice(side * CONTRIB, (side + 1) * CONTRIB)
                outgoing[kind, 2 * pair + side, 0] = real[:, span]
                outgoing[kind, 2 * pair + side, 1] = imag[:, span]
            if d:
                block_copy(kind, 2 * pair, mine).start()
                block_copy(kind, 2 * pair + 1, mine).start()
        block_copy(kind, twin, mine).start()
        incoming[kind, mine] = outgoing[kind, mine]

    for d in range(1, half):
        peer = lax.rem(mine + d, half)
        offset_copy(peer, peer).wait_recv()

    sub = lax.broadcasted_iota(jnp.int32, (subs * CONTRIB, 1), 0)
    spot = lax.broadcasted_iota(jnp.int32, (1, 2 * rows), 1)
    taper = jnp.concatenate([row_taper_ref[...], row_taper_ref[...]], axis=1)

    def row_table(column, pair):
        row_frequency = sub
        for q in range(subs):
            row_frequency = jnp.where(sub // CONTRIB == q, sub - q * CONTRIB + row_ref[q, column], row_frequency)
        start = jnp.where(spot < rows, offsets[2 * pair, :, 0:1], offsets[2 * pair + 1, :, 0:1])
        place = start + jnp.where(spot < rows, spot, spot - rows) + slab * rows
        cos, sin = cos_sin(2 * row_frequency * place)
        high, low = split(jnp.concatenate([cos * taper, sin * taper], axis=1))
        return jnp.concatenate([high, high, low], axis=1)

    def row_term(kind, table, pair):
        real = incoming[kind, pl.ds(2 * pair, 2), 0].reshape(2 * rows, CONTRIB)
        imag = incoming[kind, pl.ds(2 * pair, 2), 1].reshape(2 * rows, CONTRIB)
        high, low = split(
            jnp.concatenate([jnp.concatenate([real, imag], axis=1), jnp.concatenate([imag, -real], axis=1)], axis=0)
        )
        return dot(table, jnp.concatenate([high, low, high], axis=0))

    sources = [lax.rem(my_pair + half_pairs - d, half_pairs) for d in order]
    row_tables = [[row_table(column, pair) for pair in sources] for column in (partner, me)]
    totals = []
    for kind in range(2):
        block_copy(kind, twin, twin).wait_recv()
        totals.append(row_term(kind, row_tables[kind][-1], my_pair))
    for kind in range(2):
        total = totals[kind]
        for pair, table in zip(sources[:-1], row_tables[kind]):
            block_copy(kind, 2 * pair, 2 * pair).wait_recv()
            block_copy(kind, 2 * pair + 1, 2 * pair + 1).wait_recv()
            total = total + row_term(kind, table, pair)
        for piece in range(subs * PIECES):
            for t in range(slabs):
                start = piece // PIECES * CONTRIB + t * keep + piece % PIECES * share
                part_out[kind, t, piece] = total[start : start + share]
            for d in range(1, slabs):
                part_copy(kind, piece, lax.rem(slab + d, slabs), slab).start()

    def summed(kind, piece):
        result = part_out[kind, slab, piece]
        for d in range(1, slabs):
            peer = lax.rem(slab + d, slabs)
            part_copy(kind, piece, peer, peer).wait_recv()
            result = result + part_in[kind, peer, piece]
        return result

    for piece in range(subs * PIECES):
        cross_out[piece] = summed(0, piece)
        cross_copy(piece).start()
    sums = [summed(1, piece) for piece in range(subs * PIECES)]
    for piece in range(subs * PIECES):
        cross_copy(piece).wait_recv()
        result = (sums[piece] + cross_in[piece]) * scale
        place = slice(piece % PIECES * share, (piece % PIECES + 1) * share)
        out_buf[0, 0, piece // PIECES, place] = result[:, :CONTRIB]
        out_buf[1, 0, piece // PIECES, place] = result[:, CONTRIB:]
    out_copy = pltpu.make_async_copy(out_buf, out_ref, store)
    out_copy.start()

    for d in range(1, half):
        peer = lax.rem(mine + d, half)
        offset_copy(peer, mine).wait_send()
        for kind in range(2):
            block_copy(kind, peer, mine).wait_send()
    for piece in range(subs * PIECES):
        for kind in range(2):
            for d in range(1, slabs):
                part_copy(kind, piece, lax.rem(slab + d, slabs), slab).wait_send()
        cross_copy(piece).wait_send()
    out_copy.wait()


def solution(mesh):
    groups, slabs = mesh.shape["facet"], mesh.shape["slab"]

    def local(facets, row_taper, col_taper, facet_offsets, col_offsets, row_offsets):
        rows, width = facets.shape[1], facets.shape[2]
        subs = row_offsets.shape[1]
        keep = CONTRIB // slabs
        half = groups // 2
        pieces, share = subs * PIECES, keep // PIECES
        stacked = width // (2 * HALF) * rows
        scale = 1.0 / math.sqrt(facets.shape[0] * groups * rows * slabs * width)
        vmem = pl.BlockSpec(memory_space=pltpu.VMEM)
        smem = pl.BlockSpec(memory_space=pltpu.SMEM)
        dma = pltpu.SemaphoreType.DMA
        return pl.pallas_call(
            functools.partial(kernel, groups, slabs, scale),
            out_shape=jax.ShapeDtypeStruct((2, 1, subs, keep, CONTRIB), F32),
            in_specs=[pl.BlockSpec(memory_space=pltpu.HBM), vmem, vmem, vmem, smem, smem, smem],
            out_specs=pl.BlockSpec(memory_space=pl.ANY),
            scratch_shapes=[
                pltpu.VMEM((rows, width), F32),
                pltpu.VMEM((2, 1, subs, keep, CONTRIB), F32),
                pltpu.VMEM((stacked, 3 * HALF), BF16),
                pltpu.VMEM((stacked, 3 * HALF), BF16),
                pltpu.VMEM((2, half, 2, rows, CONTRIB), F32),
                pltpu.VMEM((2, half, 2, rows, CONTRIB), F32),
                pltpu.VMEM((half, 1, 2), jnp.int32),
                pltpu.VMEM((2, slabs, pieces, share, 2 * CONTRIB), F32),
                pltpu.VMEM((2, slabs, pieces, share, 2 * CONTRIB), F32),
                pltpu.VMEM((pieces, share, 2 * CONTRIB), F32),
                pltpu.VMEM((pieces, share, 2 * CONTRIB), F32),
                dma((CHUNKS,)), dma, dma((half,)), dma((half,)), dma((2, half)), dma((2, half)),
                dma((2, slabs, pieces)), dma((2, slabs, pieces)), dma((pieces,)), dma((pieces,)),
            ],
            compiler_params=pltpu.CompilerParams(
                collective_id=0, has_side_effects=True, vmem_limit_bytes=int(56 * 2**20)
            ),
        )(facets, row_taper.reshape(1, rows), col_taper.reshape(1, width), facet_offsets, facet_offsets, col_offsets, row_offsets.T)

    placed = (P("facet", "slab", None), P("slab"), P(), P("facet", None), P(), P())
    return jax.shard_map(
        local, mesh=mesh, in_specs=placed, out_specs=P(None, "facet", None, "slab", None), check_vma=False
    )
```

time: 25.2 us -> 23.7 us (0.940)
  Pallas kernels: 23.5 us -> 22 us
    pallas_call x1, Pallas kernels: 23.5 us -> 22 us  [local(): pl.pallas_call(functools.partial(kernel, groups, slabs, scale), out_shape...]
where the time goes in v3:
time: 23.7 us; the launch traced here: 23.5 us
  Pallas kernels  22 us (93%)
  local copies, waits for them, and re-layouts  1.47 us (6%)
    pallas_call x1, Pallas kernels, local(): pl.pallas_call(functools.partial(kernel, groups, slabs, scale), out_shape...  22 us
    unnamed x1, local copies, waits for them, and re-layouts  1.47 us

profile of v3, /device:TPU:0, one launch (start us, length us, event | category | flops | bytes accessed | tf_op | source)
XLA Modules:
  0.0 23.5 jit_solution(14523646354205188324)
XLA Ops:
  0.0 22.0 %shard_map.64 = f32[2,1,2,32,128]{4,3,2,1,0:T(8,128)} custom-call(f32[1,64,4096]{2,1,0:T(8,128)} %facet_ref.1, f32[1,64]{1,0:T(1,128)} %bitcast.5, f32[1,4096]{1,0:T(1,128)} %bitcast.3, s32[1,2]{1,0:T(1,128)} %own_offset_ref.1, s32[1,2]{1,0:T(1,128)} %own_offset_ref.1, s32[8]{0:T(128)} %col_ref.1, s32[2,8]{1,0:T(2,128)} %bitcast.4), custom_call_target="tpu_custom_call" | custom-call | tf_op jit(solution)/shard_map/pallas_call | solution.py:276
  22.0 1.5 %copy.8 = f32[2,1,2,32,128]{4,3,2,1,0:T(8,128)} copy(f32[2,1,2,32,128]{4,3,2,1,0:T(8,128)} %shard_map.64) | data formatting | bytes 131072

commit v4 on v3

--- a/solution.py
+++ b/solution.py
@@ -118,7 +118,6 @@
             ref[band, HALF : 2 * HALF] = high
             ref[band, 2 * HALF :] = low
 
-    pl.semaphore_wait(barrier, half - 1 + slabs - 1 + 1)
 
     def offset_copy(peer, home):
         return pltpu.make_async_remote_copy(
@@ -147,8 +146,6 @@
             device_id={"facet": partner}, device_id_type=MESH,
         )
 
-    for d in range(1, half):
-        offset_copy(lax.rem(mine + d, half), mine).start()
     offsets[mine] = offset_ref[...]
 
     twin = mine + 1 - 2 * lax.rem(mine, 2)
@@ -174,6 +171,10 @@
                 span = slice(side * CONTRIB, (side + 1) * CONTRIB)
                 outgoing[kind, 2 * pair + side, 0] = real[:, span]
                 outgoing[kind, 2 * pair + side, 1] = imag[:, span]
+            if not kind and d == order[0]:
+                pl.semaphore_wait(barrier, half - 1 + slabs - 1 + 1)
+                for e in range(1, half):
+                    offset_copy(lax.rem(mine + e, half), mine).start()
             if d:
                 block_copy(kind, 2 * pair, mine).start()
                 block_copy(kind, 2 * pair + 1, mine).start()

time: 23.7 us -> 23.7 us (level)
  no operation moved by 1% of the time
where the time goes in v4:
time: 23.7 us; the launch traced here: 23.5 us
  Pallas kernels  22 us (93%)
  local copies, waits for them, and re-layouts  1.47 us (6%)
    pallas_call x1, Pallas kernels, local(): pl.pallas_call(functools.partial(kernel, groups, slabs, scale), out_shape...  22 us
    unnamed x1, local copies, waits for them, and re-layouts  1.47 us

profile of v4, /device:TPU:0, one launch (start us, length us, event | category | flops | bytes accessed | tf_op | source)
XLA Modules:
  0.0 23.5 jit_solution(12584202119588878005)
XLA Ops:
  0.0 22.0 %shard_map.64 = f32[2,1,2,32,128]{4,3,2,1,0:T(8,128)} custom-call(f32[1,64,4096]{2,1,0:T(8,128)} %facet_ref.1, f32[1,64]{1,0:T(1,128)} %bitcast.5, f32[1,4096]{1,0:T(1,128)} %bitcast.3, s32[1,2]{1,0:T(1,128)} %own_offset_ref.1, s32[1,2]{1,0:T(1,128)} %own_offset_ref.1, s32[8]{0:T(128)} %col_ref.1, s32[2,8]{1,0:T(2,128)} %bitcast.4), custom_call_target="tpu_custom_call" | custom-call | tf_op jit(solution)/shard_map/pallas_call | solution.py:277
  22.0 1.5 %copy.8 = f32[2,1,2,32,128]{4,3,2,1,0:T(8,128)} copy(f32[2,1,2,32,128]{4,3,2,1,0:T(8,128)} %shard_map.64) | data formatting | bytes 131072
